TPU v7x, 32 devices: a whole 2x2x4 slice. The times are simulated.
32 devices in a mesh: layer: 4 (over x, core), row: 8 (over z, y).
Axes of the slice: x: 2, y: 2, z: 4, core: 2. Of those that a mesh axis runs over, the one named last changes fastest.
Arguments:
- magnet: float32 [3, 4, 2048, 2048], P(None, 'layer', 'row'), may hold values from -6 to 6
- kernel: float32 [7, 6, 2048, 2048], P(None, None, ('layer', 'row')), may hold values from -1.8 to 1.8, as said below
Outputs:
- demag: float32 [3, 4, 2048, 2048], P(None, 'layer', 'row')
Inputs may be any that keep to these rules, and one draw needn't show every extreme that they name: With q' = -q mod 2048 and p' = -p mod 2048: parts 0, 1, 2 satisfy kernel[o, j, q', p] = kernel[o, j, q, p'] = kernel[o, j, q, p]; part 3 changes sign under either mirror; part 4 changes sign under p -> p' and keeps it under q -> q'; part 5 keeps its sign under p -> p' and changes it under q -> q'.
All inputs are finite; a program needn't handle non-finite values.
Results may differ from a plain program's by a relative error of at most 0.0001.
Values sent between devices are 32-bit elements; how exact they have to be, the bound alone decides.
A program may use at most 256 MiB of HBM per device.

v0:
```python
import math

import jax
import jax.numpy as jnp
from jax import lax
from jax.sharding import PartitionSpec as P

high = lax.Precision.HIGH


def phases(left, right, length):
    product = left[:, None] * right[None, :] % length
    theta = product.astype(jnp.float32) * (2.0 * math.pi / length)
    return jnp.cos(theta), jnp.sin(theta)


def product_table(length):
    fine = 32
    idx = jnp.arange(length, dtype=jnp.int32)
    c1, s1 = phases(jnp.arange(length // fine, dtype=jnp.int32) * fine, idx, length)
    c2, s2 = phases(jnp.arange(fine, dtype=jnp.int32), idx, length)
    c1, s1 = c1[:, None], s1[:, None]
    cos = (c1 * c2 - s1 * s2).reshape(length, length)
    sin = (c1 * s2 + s1 * c2).reshape(length, length)
    return cos, sin


def row_table(devices, block, kept, length):
    idx = jnp.arange(length, dtype=jnp.int32)
    c1, s1 = phases(jnp.arange(devices, dtype=jnp.int32) * block, idx, length)
    c2, s2 = phases(jnp.arange(kept, dtype=jnp.int32), idx, length)
    c1, s1 = c1[:, None], s1[:, None]
    pair = jnp.stack([c1 * c2 - s1 * s2, -(c1 * s2 + s1 * c2)], axis=1)
    return pair.reshape(devices * 2 * kept, length)


def local(magnet, kernel):
    n_layer = lax.axis_size("layer")
    n_row = lax.axis_size("row")
    devices = n_row * n_layer
    n_comp, _, x_rows, y_cells = magnet.shape
    block, height = kernel.shape[2], kernel.shape[3]
    kept = block // 2 + 1
    axes = ("layer", "row")

    table = row_table(devices, block, kept, y_cells)
    cos, sin = product_table(height)

    def dot(form, a, b):
        return jnp.einsum(form, a, b, precision=high)

    spec_r, spec_i = [], []
    for c in range(n_comp):
        rows = dot("qy,xy->qx", table, magnet[c, 0])
        moved = lax.all_to_all(
            rows.reshape(devices, 2 * kept, x_rows), axes, split_axis=0, concat_axis=0, tiled=True
        )
        split = moved.reshape(n_layer, n_row, 2, kept, x_rows)
        flat = jnp.transpose(split, (2, 0, 3, 1, 4)).reshape(2 * n_layer * kept, height)
        by_cos = dot("mx,xp->mp", flat, cos).reshape(2, n_layer, kept, height)
        by_sin = dot("mx,xp->mp", flat, sin).reshape(2, n_layer, kept, height)
        spec_r.append(by_cos[0] + by_sin[1])
        spec_i.append(by_cos[1] - by_sin[0])

    row_idx = jnp.arange(kept, dtype=jnp.int32)
    edge = (row_idx == 0) | (row_idx == kept - 1)
    weight = jnp.where(edge, -1.0, -2.0)[:, None] * (1.0 / (height * y_cells))
    coeffs = kernel[:, :, :kept]

    entries = (
        ((0, False), (3, False), (4, True)),
        ((3, False), (1, False), (5, True)),
        ((4, True), (5, True), (2, False)),
    )
    outs = []
    for c in range(n_comp):
        real_rows, imag_rows = [], []
        for target in range(n_layer):
            total_r, total_i = 0.0, 0.0
            for source in range(n_layer):
                offset = target - source + n_layer - 1
                for c2 in range(n_comp):
                    part, turned = entries[c][c2]
                    k = coeffs[offset, part]
                    re, im = spec_r[c2][source], spec_i[c2][source]
                    if turned:
                        total_r = total_r - k * im
                        total_i = total_i + k * re
                    else:
                        total_r = total_r + k * re
                        total_i = total_i + k * im
            real_rows.append(total_r * weight)
            imag_rows.append(total_i * weight)
        field = jnp.stack([jnp.stack(real_rows), jnp.stack(imag_rows)])
        flat = field.reshape(2 * n_layer * kept, height)
        by_cos = dot("mp,px->mx", flat, cos).reshape(2, n_layer, kept, n_row, x_rows)
        by_sin = dot("mp,px->mx", flat, sin).reshape(2, n_layer, kept, n_row, x_rows)
        cells = jnp.stack([by_cos[0] - by_sin[1], by_cos[1] + by_sin[0]], axis=2)
        cells = jnp.transpose(cells, (0, 3, 2, 1, 4)).reshape(devices, 2 * kept, x_rows)
        back = lax.all_to_all(cells, axes, split_axis=0, concat_axis=0, tiled=True)
        outs.append(dot("qx,qy->xy", back.reshape(devices * 2 * kept, x_rows), table))
    return jnp.stack(outs)[:, None]


def solution(mesh):
    in_specs = (P(None, "layer", "row", None), P(None, None, ("layer", "row"), None))
    out_specs = P(None, "layer", "row", None)
    return jax.shard_map(local, mesh=mesh, in_specs=in_specs, out_specs=out_specs, check_vma=False)
```

profile of v0, /device:TPU:13, one launch (start us, length us, event | category | flops | bytes accessed | tf_op | source)
XLA Modules:
  0.0 522.2 jit_solution(2787242964980262460)
XLA Ops:
  7.4 5.0 pad_maximum_fusion
  12.4 10.9 %fusion = f32[32,66,256]{2,0,1:T(8,128)S(1)} fusion(f32[32,66,2048]{2,0,1:T(8,128)S(1)} %bitcast.2210, f32[3,1,256,2048]{3,2,1,0:T(8,128)} %param.2), kind=kOutput, calls=%fused_computation.15 | convolution fusion | flops 6643777536 | bytes 21561344 | tf_op jit(solution)/shard_map/qy,xy->qx/dot_general | solution.py:50
  26.0 6.6 %all-to-all-start.2 = ((f32[32,66,256]{2,1,0:T(8,128)}), f32[32,66,256]{2,1,0:T(8,128)S(1)}, u32[]{:S(2)}, u32[]{:S(2)}) async-start(f32[32,66,256]{2,1,0:T(8,128)} %copy.44), calls=%async_computation.2 | async-start | bytes 4718592 | tf_op jit(solution)/shard_map/all_to_all | solution.py:55
  32.6 10.8 %fusion.2 = f32[32,66,256]{2,0,1:T(8,128)S(1)} fusion(f32[32,66,2048]{2,0,1:T(8,128)} %bitcast.2211, f32[3,1,256,2048]{3,2,1,0:T(8,128)} %param.2), kind=kOutput, calls=%fused_computation.17 | convolution fusion | flops 6643777536 | bytes 21561344 | tf_op jit(solution)/shard_map/qy,xy->qx/dot_general | solution.py:50
  46.1 37.6 %all-to-all-done.2 = f32[32,66,256]{2,1,0:T(8,128)S(1)} async-done(((f32[32,66,256]{2,1,0:T(8,128)}), f32[32,66,256]{2,1,0:T(8,128)S(1)}, u32[]{:S(2)}, u32[]{:S(2)}) %all-to-all-start.2) | async-done | bytes 2162720 | tf_op jit(solution)/shard_map/all_to_all | solution.py:55
  83.7 7.9 %all-to-all-start.1 = ((f32[32,66,256]{2,1,0:T(8,128)}), f32[32,66,256]{2,1,0:T(8,128)}, u32[]{:S(2)}, u32[]{:S(2)}) async-start(f32[32,66,256]{2,1,0:T(8,128)} %copy.41), calls=%async_computation.1 | async-start | bytes 4718592 | tf_op jit(solution)/shard_map/all_to_all | solution.py:55
  91.6 10.8 %fusion.4 = f32[32,66,256]{2,0,1:T(8,128)S(1)} fusion(f32[32,66,2048]{2,0,1:T(8,128)} %bitcast.2212, f32[3,1,256,2048]{3,2,1,0:T(8,128)} %param.2), kind=kOutput, calls=%fused_computation.19 | convolution fusion | flops 6643777536 | bytes 21561344 | tf_op jit(solution)/shard_map/qy,xy->qx/dot_general | solution.py:50
  109.0 33.8 %all-to-all-done.1 = f32[32,66,256]{2,1,0:T(8,128)} async-done(((f32[32,66,256]{2,1,0:T(8,128)}), f32[32,66,256]{2,1,0:T(8,128)}, u32[]{:S(2)}, u32[]{:S(2)}) %all-to-all-start.1) | async-done | bytes 2162720 | tf_op jit(solution)/shard_map/all_to_all | solution.py:55
  142.8 8.4 %all-to-all-start = ((f32[32,66,256]{2,1,0:T(8,128)}), f32[32,66,256]{2,1,0:T(8,128)}, u32[]{:S(2)}, u32[]{:S(2)}) async-start(f32[32,66,256]{2,1,0:T(8,128)} %copy.38), calls=%async_computation | async-start | bytes 4718592 | tf_op jit(solution)/shard_map/all_to_all | solution.py:55
  151.2 8.8 %multiply_subtract_fusion = (f32[64,32,2048]{2,1,0:T(8,128)S(1)}, f32[64,32,2048]{2,1,0:T(8,128)}) fusion(f32[32,2048]{1,0:T(8,128)} %get-tuple-element.27, f32[64,2048]{1,0:T(8,128)S(1)} %get-tuple-element.22, f32[32,2048]{1,0:T(8,128)} %get-tuple-element.28, f32[64,2048]{1,0:T(8,128)S(1)} %get-tuple-element.21), kind=kLoop, calls=%fused_computation.2 | loop fusion | flops 25165824 | bytes 35127296 | tf_op jit(solution)/shard_map/sub | solution.py:23
  167.1 11.8 %fusion.339 = f32[264,2048]{1,0:T(8,128)S(1)} fusion(f32[264,2048]{1,0:T(8,128)S(1)} %bitcast.2217, f32[2048,2048]{1,0:T(8,128)} %bitcast.2204), kind=kOutput, calls=%fused_computation.699 | convolution fusion | flops 6643777536 | bytes 21102592 | tf_op jit(solution)/shard_map/mx,xp->mp/dot_general | solution.py:50
  178.9 9.4 %fusion.338 = f32[264,2048]{1,0:T(8,128)} fusion(f32[264,2048]{1,0:T(8,128)S(1)} %bitcast.2218, f32[2048,2048]{1,0:T(8,128)S(1)} %bitcast.2196), kind=kOutput, calls=%fused_computation.698 | convolution fusion | flops 6643777536 | bytes 21102592 | tf_op jit(solution)/shard_map/mx,xp->mp/dot_general | solution.py:50
  188.3 12.8 %fusion.337 = f32[264,2048]{1,0:T(8,128)} fusion(f32[264,2048]{1,0:T(8,128)S(1)} %bitcast.2219, f32[2048,2048]{1,0:T(8,128)} %bitcast.2205), kind=kOutput, calls=%fused_computation.697 | convolution fusion | flops 6643777536 | bytes 21102592 | tf_op jit(solution)/shard_map/mx,xp->mp/dot_general | solution.py:50
  201.1 9.3 %fusion.336 = f32[264,2048]{1,0:T(8,128)} fusion(f32[264,2048]{1,0:T(8,128)S(1)} %bitcast.2220, f32[2048,2048]{1,0:T(8,128)S(1)} %bitcast.2197), kind=kOutput, calls=%fused_computation.696 | convolution fusion | flops 6643777536 | bytes 21102592 | tf_op jit(solution)/shard_map/mx,xp->mp/dot_general | solution.py:50
  214.1 13.0 %fusion.335 = f32[264,2048]{1,0:T(8,128)} fusion(f32[264,2048]{1,0:T(8,128)S(1)} %bitcast.2221, f32[2048,2048]{1,0:T(8,128)} %bitcast.2206), kind=kOutput, calls=%fused_computation.695 | convolution fusion | flops 6643777536 | bytes 21102592 | tf_op jit(solution)/shard_map/mx,xp->mp/dot_general | solution.py:50
  227.2 9.3 %fusion.334 = f32[264,2048]{1,0:T(8,128)} fusion(f32[264,2048]{1,0:T(8,128)S(1)} %bitcast.2222, f32[2048,2048]{1,0:T(8,128)S(1)} %bitcast.2203), kind=kOutput, calls=%fused_computation.694 | convolution fusion | flops 6643777536 | bytes 21102592 | tf_op jit(solution)/shard_map/mx,xp->mp/dot_general | solution.py:50
  274.4 15.3 %fusion.341 = f32[264,2048]{1,0:T(8,128)} fusion(f32[264,2048]{1,0:T(8,128)} %reshape.1004, f32[2048,2048]{1,0:T(8,128)} %bitcast.2207), kind=kOutput, calls=%fused_computation.701 | convolution fusion | flops 6643777536 | bytes 21102592 | tf_op jit(solution)/shard_map/mp,px->mx/dot_general | solution.py:50
  289.7 12.7 %fusion.340 = f32[264,2048]{1,0:T(8,128)} fusion(f32[264,2048]{1,0:T(8,128)S(1)} %copy-done.10, f32[2048,2048]{1,0:T(8,128)} %bitcast.2198), kind=kOutput, calls=%fused_computation.700 | convolution fusion | flops 6643777536 | bytes 21102592 | tf_op jit(solution)/shard_map/mp,px->mx/dot_general | solution.py:50
  315.6 6.3 %all-to-all-start.3 = ((f32[32,66,256]{2,1,0:T(8,128)}), f32[32,66,256]{2,1,0:T(8,128)}, u32[]{:S(2)}, u32[]{:S(2)}) async-start(f32[32,66,256]{2,1,0:T(8,128)} %copy.49), calls=%async_computation.3 | async-start | bytes 4718592 | tf_op jit(solution)/shard_map/all_to_all | solution.py:100
  321.9 12.2 %fusion.345 = f32[264,2048]{1,0:T(8,128)S(1)} fusion(f32[264,2048]{1,0:T(8,128)} %reshape.1011, f32[2048,2048]{1,0:T(8,128)} %bitcast.2208), kind=kOutput, calls=%fused_computation.705 | convolution fusion | flops 6643777536 | bytes 21102592 | tf_op jit(solution)/shard_map/mp,px->mx/dot_general | solution.py:50
  334.2 12.0 %fusion.344 = f32[264,2048]{1,0:T(8,128)S(1)} fusion(f32[264,2048]{1,0:T(8,128)S(1)} %copy-done.9, f32[2048,2048]{1,0:T(8,128)} %bitcast.2199), kind=kOutput, calls=%fused_computation.704 | convolution fusion | flops 6643777536 | bytes 21102592 | tf_op jit(solution)/shard_map/mp,px->mx/dot_general | solution.py:50
  360.0 12.9 %all-to-all-done.3 = f32[32,66,256]{2,1,0:T(8,128)} async-done(((f32[32,66,256]{2,1,0:T(8,128)}), f32[32,66,256]{2,1,0:T(8,128)}, u32[]{:S(2)}, u32[]{:S(2)}) %all-to-all-start.3) | async-done | bytes 2162720 | tf_op jit(solution)/shard_map/all_to_all | solution.py:100
  372.9 8.4 %all-to-all-start.5 = ((f32[32,66,256]{2,1,0:T(8,128)}), f32[32,66,256]{2,1,0:T(8,128)}, u32[]{:S(2)}, u32[]{:S(2)}) async-start(f32[32,66,256]{2,1,0:T(8,128)} %copy.56), calls=%async_computation.5 | async-start | bytes 4718592 | tf_op jit(solution)/shard_map/all_to_all | solution.py:100
  392.0 11.4 %fusion.343 = f32[264,2048]{1,0:T(8,128)S(1)} fusion(f32[264,2048]{1,0:T(8,128)S(1)} %reshape.1008, f32[2048,2048]{1,0:T(8,128)} %bitcast.2209), kind=kOutput, calls=%fused_computation.703 | convolution fusion | flops 6643777536 | bytes 21102592 | tf_op jit(solution)/shard_map/mp,px->mx/dot_general | solution.py:50
  403.5 11.6 %fusion.342 = f32[264,2048]{1,0:T(8,128)S(1)} fusion(f32[264,2048]{1,0:T(8,128)S(1)} %reshape.1008, f32[2048,2048]{1,0:T(8,128)} %bitcast.2200), kind=kOutput, calls=%fused_computation.702 | convolution fusion | flops 6643777536 | bytes 21102592 | tf_op jit(solution)/shard_map/mp,px->mx/dot_general | solution.py:50
  419.6 12.6 %all-to-all-done.5 = f32[32,66,256]{2,1,0:T(8,128)} async-done(((f32[32,66,256]{2,1,0:T(8,128)}), f32[32,66,256]{2,1,0:T(8,128)}, u32[]{:S(2)}, u32[]{:S(2)}) %all-to-all-start.5) | async-done | bytes 2162720 | tf_op jit(solution)/shard_map/all_to_all | solution.py:100
  432.2 7.3 %all-to-all-start.4 = ((f32[32,66,256]{2,1,0:T(8,128)}), f32[32,66,256]{2,1,0:T(8,128)S(1)}, u32[]{:S(2)}, u32[]{:S(2)}) async-start(f32[32,66,256]{2,1,0:T(8,128)} %copy.53), calls=%async_computation.4 | async-start | bytes 4718592 | tf_op jit(solution)/shard_map/all_to_all | solution.py:100
  439.6 21.0 %copy.50 = f32[32,2,33,2048]{3,2,1,0:T(8,128)} copy(f32[32,2,33,2048]{3,0,2,1:T(8,128)} %copy-done.1) | data formatting | bytes 34603008 | tf_op jit(solution)/shard_map/stack | solution.py:33
  460.6 15.1 %reshape.1007 = f32[2112,2048]{1,0:T(8,128)} reshape(f32[32,2,33,2048]{3,2,1,0:T(8,128)} %copy.50) | data formatting | bytes 34603008 | tf_op jit(solution)/shard_map/reshape | solution.py:34
  481.2 13.8 %convolution_bitcast_fusion.2 = f32[1,256,2048]{2,1,0:T(8,128)} fusion(f32[2112,256]{1,0:T(8,128)} %reshape.1006, f32[2112,2048]{1,0:T(8,128)} %reshape.1007), kind=kOutput, calls=%fused_computation.8 | convolution fusion | flops 6643777536 | bytes 21561344 | tf_op jit(solution)/shard_map/qx,qy->xy/dot_general | solution.py:50
  495.0 10.4 %convolution_bitcast_fusion = f32[1,256,2048]{2,1,0:T(8,128)} fusion(f32[2112,256]{1,0:T(8,128)S(1)} %copy-done.14, f32[2112,2048]{1,0:T(8,128)S(1)} %copy-done.2), kind=kOutput, calls=%fused_computation.6 | convolution fusion | flops 6643777536 | bytes 21561344 | tf_op jit(solution)/shard_map/qx,qy->xy/dot_general | solution.py:50
  506.9 11.5 %convolution_bitcast_fusion.1 = f32[1,256,2048]{2,1,0:T(8,128)S(1)} fusion(f32[2112,256]{1,0:T(8,128)} %reshape.1010, f32[2112,2048]{1,0:T(8,128)} %reshape.1007), kind=kOutput, calls=%fused_computation.7 | convolution fusion | flops 6643777536 | bytes 21561344 | tf_op jit(solution)/shard_map/qx,qy->xy/dot_general | solution.py:50
  (180 shorter events, 119.9 us)
Async XLA Ops:
  26.0 57.7 %all-to-all-start.2 = ((f32[32,66,256]{2,1,0:T(8,128)}), f32[32,66,256]{2,1,0:T(8,128)S(1)}, u32[]{:S(2)}, u32[]{:S(2)}) async-start(f32[32,66,256]{2,1,0:T(8,128)} %copy.44), calls=%async_computation.2 | async-start | bytes 4718592 | tf_op jit(solution)/shard_map/all_to_all | solution.py:55
  83.7 59.0 %all-to-all-start.1 = ((f32[32,66,256]{2,1,0:T(8,128)}), f32[32,66,256]{2,1,0:T(8,128)}, u32[]{:S(2)}, u32[]{:S(2)}) async-start(f32[32,66,256]{2,1,0:T(8,128)} %copy.41), calls=%async_computation.1 | async-start | bytes 4718592 | tf_op jit(solution)/shard_map/all_to_all | solution.py:55
  142.8 67.7 %all-to-all-start = ((f32[32,66,256]{2,1,0:T(8,128)}), f32[32,66,256]{2,1,0:T(8,128)}, u32[]{:S(2)}, u32[]{:S(2)}) async-start(f32[32,66,256]{2,1,0:T(8,128)} %copy.38), calls=%async_computation | async-start | bytes 4718592 | tf_op jit(solution)/shard_map/all_to_all | solution.py:55
  160.0 41.1 %copy-start = (f32[64,32,2048]{2,1,0:T(8,128)}, f32[64,32,2048]{2,1,0:T(8,128)S(1)}, u32[]{:S(2)}) copy-start(f32[64,32,2048]{2,1,0:T(8,128)S(1)} %get-tuple-element.17) | copy-start | bytes 50331652
  210.5 16.7 %slice-start = ((s8[16777216]{0:T(1024)(128)(4,1)}), s8[4194304]{0:T(1024)(128)(4,1)S(1)}, s32[]{:S(2)}) async-start(s8[16777216]{0:T(1024)(128)(4,1)} %bitcast.2201), calls=%async_computation.6 | async-start | bytes 8388608
  213.0 14.2 %slice-start.1 = ((s8[16777216]{0:T(1024)(128)(4,1)}), s8[4194304]{0:T(1024)(128)(4,1)S(1)}, s32[]{:S(2)}) async-start(s8[16777216]{0:T(1024)(128)(4,1)} %bitcast.2201), calls=%async_computation.7 | async-start | bytes 8388608
  214.1 13.1 %slice-start.2 = ((s8[16777216]{0:T(1024)(128)(4,1)}), s8[4194304]{0:T(1024)(128)(4,1)S(1)}, s32[]{:S(2)}) async-start(s8[16777216]{0:T(1024)(128)(4,1)} %bitcast.2201), calls=%async_computation.8 | async-start | bytes 8388608
  214.1 13.1 %slice-start.3 = ((s8[16777216]{0:T(1024)(128)(4,1)}), s8[4194304]{0:T(1024)(128)(4,1)S(1)}, s32[]{:S(2)}) async-start(s8[16777216]{0:T(1024)(128)(4,1)} %bitcast.2201), calls=%async_computation.9 | async-start | bytes 8388608
  227.2 11.4 %copy-start.12 = (f32[264,2048]{1,0:T(8,128)S(1)}, f32[264,2048]{1,0:T(8,128)}, u32[]{:S(2)}) copy-start(f32[264,2048]{1,0:T(8,128)} %fusion.336) | copy-start | bytes 6488068
  236.5 18.5 %slice-start.4 = ((s8[22020096]{0:T(1024)(128)(4,1)}), s8[4194304]{0:T(1024)(128)(4,1)S(1)}, s32[]{:S(2)}) async-start(s8[22020096]{0:T(1024)(128)(4,1)} %bitcast.2213), calls=%async_computation.10 | async-start | bytes 8388608
  238.8 20.5 %copy-start.3 = (f32[132,2048]{1,0:T(8,128)}, f32[132,2048]{1,0:T(8,128)S(1)}, u32[]{:S(2)}) copy-start(f32[132,2048]{1,0:T(8,128)S(1)} %get-tuple-element.11) | copy-start | bytes 3244036
  238.8 16.2 %slice-start.5 = ((s8[22020096]{0:T(1024)(128)(4,1)}), s8[4194304]{0:T(1024)(128)(4,1)S(1)}, s32[]{:S(2)}) async-start(s8[22020096]{0:T(1024)(128)(4,1)} %bitcast.2213), calls=%async_computation.11 | async-start | bytes 8388608
  241.1 18.3 %copy-start.5 = (f32[132,2048]{1,0:T(8,128)}, f32[132,2048]{1,0:T(8,128)S(1)}, u32[]{:S(2)}) copy-start(f32[132,2048]{1,0:T(8,128)S(1)} %get-tuple-element.13) | copy-start | bytes 3244036
  241.1 14.0 %slice-start.6 = ((s8[22020096]{0:T(1024)(128)(4,1)}), s8[4194304]{0:T(1024)(128)(4,1)S(1)}, s32[]{:S(2)}) async-start(s8[22020096]{0:T(1024)(128)(4,1)} %bitcast.2213), calls=%async_computation.12 | async-start | bytes 8388608
  243.7 15.7 %copy-start.7 = (f32[132,2048]{1,0:T(8,128)}, f32[132,2048]{1,0:T(8,128)S(1)}, u32[]{:S(2)}) copy-start(f32[132,2048]{1,0:T(8,128)S(1)} %get-tuple-element.15) | copy-start | bytes 3244036
  243.7 11.4 %slice-start.7 = ((s8[22020096]{0:T(1024)(128)(4,1)}), s8[4194304]{0:T(1024)(128)(4,1)S(1)}, s32[]{:S(2)}) async-start(s8[22020096]{0:T(1024)(128)(4,1)} %bitcast.2213), calls=%async_computation.13 | async-start | bytes 8388608
  274.4 15.3 %copy-start.10 = (f32[264,2048]{1,0:T(8,128)S(1)}, f32[264,2048]{1,0:T(8,128)}, u32[]{:S(2)}) copy-start(f32[264,2048]{1,0:T(8,128)} %reshape.1004) | copy-start | bytes 6488068
  289.7 12.8 %copy-start.18 = (f32[1,33,2048]{2,1,0:T(8,128)S(1)}, f32[1,33,2048]{2,1,0:T(8,128)}, u32[]{:S(2)}) copy-start(f32[1,33,2048]{2,1,0:T(8,128)} %fusion.85) | copy-start | bytes 811012
  289.7 12.8 %copy-start.19 = (f32[1,33,2048]{2,1,0:T(8,128)S(1)}, f32[1,33,2048]{2,1,0:T(8,128)}, u32[]{:S(2)}) copy-start(f32[1,33,2048]{2,1,0:T(8,128)} %fusion.72) | copy-start | bytes 811012
  289.7 12.8 %copy-start.20 = (f32[1,33,2048]{2,1,0:T(8,128)S(1)}, f32[1,33,2048]{2,1,0:T(8,128)}, u32[]{:S(2)}) copy-start(f32[1,33,2048]{2,1,0:T(8,128)} %fusion.50) | copy-start | bytes 811012
  289.7 12.8 %copy-start.21 = (f32[1,33,2048]{2,1,0:T(8,128)S(1)}, f32[1,33,2048]{2,1,0:T(8,128)}, u32[]{:S(2)}) copy-start(f32[1,33,2048]{2,1,0:T(8,128)} %fusion.28) | copy-start | bytes 811012
  315.6 57.3 %all-to-all-start.3 = ((f32[32,66,256]{2,1,0:T(8,128)}), f32[32,66,256]{2,1,0:T(8,128)}, u32[]{:S(2)}, u32[]{:S(2)}) async-start(f32[32,66,256]{2,1,0:T(8,128)} %copy.49), calls=%async_computation.3 | async-start | bytes 4718592 | tf_op jit(solution)/shard_map/all_to_all | solution.py:100
  321.9 12.2 %copy-start.9 = (f32[264,2048]{1,0:T(8,128)S(1)}, f32[264,2048]{1,0:T(8,128)}, u32[]{:S(2)}) copy-start(f32[264,2048]{1,0:T(8,128)} %reshape.1011) | copy-start | bytes 6488068
  334.2 16.7 %slice-start.10 = ((s8[22020096]{0:T(1024)(128)(4,1)}), s8[1048576]{0:T(1024)(128)(4,1)S(1)}, s32[]{:S(2)}) async-start(s8[22020096]{0:T(1024)(128)(4,1)} %bitcast.2215), calls=%async_computation.16 | async-start | bytes 2097152
  334.2 16.7 %slice-start.11 = ((s8[22020096]{0:T(1024)(128)(4,1)}), s8[4194304]{0:T(1024)(128)(4,1)S(1)}, s32[]{:S(2)}) async-start(s8[22020096]{0:T(1024)(128)(4,1)} %bitcast.2215), calls=%async_computation.17 | async-start | bytes 8388608
  334.2 16.7 %slice-start.12 = ((s8[22020096]{0:T(1024)(128)(4,1)}), s8[4194304]{0:T(1024)(128)(4,1)S(1)}, s32[]{:S(2)}) async-start(s8[22020096]{0:T(1024)(128)(4,1)} %bitcast.2215), calls=%async_computation.18 | async-start | bytes 8388608
  372.9 59.4 %all-to-all-start.5 = ((f32[32,66,256]{2,1,0:T(8,128)}), f32[32,66,256]{2,1,0:T(8,128)}, u32[]{:S(2)}, u32[]{:S(2)}) async-start(f32[32,66,256]{2,1,0:T(8,128)} %copy.56), calls=%async_computation.5 | async-start | bytes 4718592 | tf_op jit(solution)/shard_map/all_to_all | solution.py:100
  432.2 73.2 %all-to-all-start.4 = ((f32[32,66,256]{2,1,0:T(8,128)}), f32[32,66,256]{2,1,0:T(8,128)S(1)}, u32[]{:S(2)}, u32[]{:S(2)}) async-start(f32[32,66,256]{2,1,0:T(8,128)} %copy.53), calls=%async_computation.4 | async-start | bytes 4718592 | tf_op jit(solution)/shard_map/all_to_all | solution.py:100
  481.2 13.8 %copy-start.2 = (f32[2112,2048]{1,0:T(8,128)S(1)}, f32[2112,2048]{1,0:T(8,128)}, u32[]{:S(2)}) copy-start(f32[2112,2048]{1,0:T(8,128)} %reshape.1007) | copy-start | bytes 51904516
  481.2 13.8 %copy-start.14 = (f32[2112,256]{1,0:T(8,128)S(1)}, f32[2112,256]{1,0:T(8,128)}, u32[]{:S(2)}) copy-start(f32[2112,256]{1,0:T(8,128)} %reshape.1013) | copy-start | bytes 6488068
  506.9 11.6 %copy-start.15 = (f32[1,256,2048]{2,1,0:T(8,128)S(1)}, f32[1,256,2048]{2,1,0:T(8,128)}, u32[]{:S(2)}) copy-start(f32[1,256,2048]{2,1,0:T(8,128)} %convolution_bitcast_fusion.2) | copy-start | bytes 6291460
  506.9 11.6 %copy-start.16 = (f32[1,256,2048]{2,1,0:T(8,128)S(1)}, f32[1,256,2048]{2,1,0:T(8,128)}, u32[]{:S(2)}) copy-start(f32[1,256,2048]{2,1,0:T(8,128)} %convolution_bitcast_fusion) | copy-start | bytes 6291460
  (18 other events, 63.3 us)
where the time goes:
time: 527 us; the launch traced here: 522 us
  matrix products  209 us (40%)
  waiting for transfers between devices  96.9 us (18%)
  local copies, waits for them, and re-layouts  88.3 us (17%)
  other arithmetic  81.6 us (15%)
  starting transfers between devices  44.9 us (9%)
    dot_general x18, matrix products, dot(): return jnp.einsum(form, a, b, precision=high)  209 us
    all_to_all x3, waiting for transfers between devices, local(): lax.all_to_all(rows.reshape(devices, 2 * kept, x_rows), axes, split_axis=...  71.4 us
    all_to_all x3, waiting for transfers between devices, local(): back = lax.all_to_all(cells, axes, split_axis=0, concat_axis=0, tiled=True)  25.5 us
    mul x12, other arithmetic, local(): real_rows.append(total_r * weight)  25 us
    all_to_all x3, starting transfers between devices, local(): lax.all_to_all(rows.reshape(devices, 2 * kept, x_rows), axes, split_axis=...  22.9 us
    all_to_all x3, starting transfers between devices, local(): back = lax.all_to_all(cells, axes, split_axis=0, concat_axis=0, tiled=True)  22 us
    another operation x1, local copies, waits for them, and re-layouts, row_table(): pair = jnp.stack([c1 * c2 - s1 * s2, -(c1 * s2 + s1 * c2)], axis=1)  21 us
    reshape x1, local copies, waits for them, and re-layouts, row_table(): return pair.reshape(devices * 2 * kept, length)  15.1 us
  transfers between devices with their start and end apart: 6, of which 4 were waited for; matrix products, arithmetic and copies ran while one was open for 44% of the time, Pallas kernels for 0%

commit v1 on v0

--- a/solution.py
+++ b/solution.py
@@ -1,9 +1,17 @@
+import functools
 import math
 
 import jax
 import jax.numpy as jnp
+import numpy as np
 from jax import lax
+from jax.experimental import pallas as pl
+from jax.experimental.pallas import tpu as pltpu
 from jax.sharding import PartitionSpec as P
+
+MESH = pl.DeviceIdType.MESH
+SUB, LANE = 8, 128
+bf16, f32 = jnp.bfloat16, jnp.float32
 
 high = lax.Precision.HIGH
 
@@ -34,7 +42,7 @@
     return pair.reshape(devices * 2 * kept, length)
 
 
-def local(magnet, kernel):
+def general(magnet, kernel):
     n_layer = lax.axis_size("layer")
     n_row = lax.axis_size("row")
     devices = n_row * n_layer
@@ -102,6 +110,446 @@
     return jnp.stack(outs)[:, None]
 
 
+def wave(angles, length, half):
+    product = np.outer(angles, np.arange(half)) % length
+    theta = product * (2.0 * np.pi / length)
+    return np.stack([np.cos(theta), np.sin(theta)])
+
+
+def base_tables(block, kept, devices, length):
+    half = length // 2
+    fine = 32
+    coarse = wave(np.arange(half // fine) * fine, length, half)
+    small = wave(np.arange(fine), length, half)
+    low = np.arange(kept)
+    low[0] = kept
+    flip = (-1.0) ** np.arange(half)
+    rows = np.stack([wave(low, length, half), wave(np.arange(kept), length, half) * flip])
+    return coarse.astype(np.float32), small.astype(np.float32), rows.astype(np.float32)
+
+
+def split(x):
+    hi = x.astype(bf16)
+    return hi, (x - hi.astype(f32)).astype(bf16)
+
+
+def dot(a, b):
+    return jnp.dot(a, b, preferred_element_type=f32)
+
+
+def dot_t(a, b):
+    return lax.dot_general(a, b, (((1,), (1,)), ((), ())), preferred_element_type=f32)
+
+
+def fused_kernel(
+    dims, mag_ref, ker_ref, coarse, small, rowt, out_ref,
+    acc, mhi, mlo, fs, fr, br, thi, tlo, lhi, llo, kre, kim, kmid, kzero, ahi, alo, z, bhi, blo, wsc,
+    mag_sem, k_sem, kmid_sem, zero_send, zero_recv, fsend, frecv, bsend, brecv, out_sem,
+):
+    n_layer, n_row, n_comp, x_rows, n_y, kept, n_chunk = dims
+    devices = n_layer * n_row
+    half = n_y // 2
+    hrow = n_row // 2
+    hdev = devices // 2
+    step = half // hdev // 32
+    group = 2 * SUB * n_comp
+    m_rows = n_layer * group
+    n_tile = half // LANE
+    l = lax.axis_index("layer")
+    r = lax.axis_index("row")
+    me = l * n_row + r
+
+    def at(d):
+        return (d // n_row, d % n_row)
+
+    barrier = pltpu.get_barrier_semaphore()
+
+    def greet(k, _):
+        pl.semaphore_signal(barrier, inc=1, device_id=at((me + k) % devices), device_id_type=MESH)
+        return 0
+
+    lax.fori_loop(1, devices, greet, 0)
+
+    def mag_copy(c):
+        return pltpu.make_async_copy(mag_ref.at[c, 0], acc.at[c], mag_sem.at[c])
+
+    def k_copy(j):
+        src = ker_ref.at[:, pl.ds(pl.multiple_of(j * SUB, SUB), SUB), pl.ds(0, half + LANE)]
+        return pltpu.make_async_copy(src, kre.at[:, :, pl.ds(0, half + LANE)], k_sem)
+
+    for c in range(n_comp):
+        mag_copy(c).start()
+    k_copy(0).start()
+    mid_copy = pltpu.make_async_copy(ker_ref.at[:, pl.ds(kept, SUB), pl.ds(0, half + LANE)], kmid, kmid_sem)
+    mid_copy.start()
+    zero_copy = pltpu.make_async_remote_copy(
+        src_ref=ker_ref.at[:, pl.ds(0, SUB), pl.ds(0, half + LANE)], dst_ref=kzero,
+        send_sem=zero_send, recv_sem=zero_recv, device_id=at((me + hdev) % devices), device_id_type=MESH,
+    )
+
+    sub = lax.broadcasted_iota(jnp.int32, (SUB, half), 0)
+    odd_row = jnp.where(sub % 2 == 0, 1.0, -1.0).astype(f32)
+
+    def build_rows(j):
+        rows = pl.ds(pl.multiple_of(j * SUB, SUB), SUB)
+
+        def body(e, _):
+            c1 = coarse[0, pl.ds(e * step, 1), :]
+            s1 = coarse[1, pl.ds(e * step, 1), :]
+            for v in range(2):
+                c2 = rowt[v, 0, rows, :]
+                s2 = rowt[v, 1, rows, :]
+                top = c1 * c2 - s1 * s2
+                low = -(s1 * c2 + c1 * s2)
+                if v == 1:
+                    packed = jnp.logical_and(sub == 0, jnp.logical_and(e == 0, j == 0))
+                    low = jnp.where(packed, 1.0, low)
+                both = jnp.concatenate([top, low], axis=0)
+                sign = jnp.concatenate([odd_row, odd_row], axis=0)
+                hi, lo = split(both)
+                at_row = pl.ds(pl.multiple_of((v * hdev + e) * 2 * SUB, 2 * SUB), 2 * SUB)
+                lhi[at_row, 0:half] = hi
+                llo[at_row, 0:half] = lo
+                lhi[at_row, half : 2 * half] = (hi.astype(f32) * sign).astype(bf16)
+                llo[at_row, half : 2 * half] = (lo.astype(f32) * sign).astype(bf16)
+            return 0
+
+        lax.fori_loop(0, hdev, body, 0)
+
+    def first(j, _):
+        build_rows(j)
+        for c in range(n_comp):
+
+            @pl.when(j == 0)
+            def _():
+                mag_copy(c).wait()
+
+                def body(i, _):
+                    rows = pl.ds(pl.multiple_of(i * 16, 16), 16)
+                    hi, lo = split(acc[c, rows, :])
+                    mhi[c, rows, :] = hi
+                    mlo[c, rows, :] = lo
+                    return 0
+
+                lax.fori_loop(0, x_rows // 16, body, 0)
+
+            value = dot_t(lhi[...], mhi[c]) + dot_t(llo[...], mhi[c]) + dot_t(lhi[...], mlo[c])
+            fs[j, c] = value.reshape(devices, 2 * SUB, x_rows)
+
+            if c == 0:
+
+                @pl.when(j == 0)
+                def _():
+                    pl.semaphore_wait(barrier, devices - 1)
+
+                    @pl.when(me == 0)
+                    def _():
+                        zero_copy.start()
+
+            def send(k, _):
+                d = (me + k) % devices
+                pltpu.make_async_remote_copy(
+                    src_ref=fs.at[j, c, d], dst_ref=fr.at[j, c, me], send_sem=fsend.at[j, c], recv_sem=frecv.at[j, c],
+                    device_id=at(d), device_id_type=MESH,
+                ).start()
+                return 0
+
+            lax.fori_loop(1, devices, send, 0)
+            fr[j, c, me] = fs[j, c, me]
+        return 0
+
+    lax.fori_loop(0, n_chunk, first, 0)
+
+    def build_square(a, _):
+        c1 = coarse[0, pl.ds(a, 1), :]
+        s1 = coarse[1, pl.ds(a, 1), :]
+        for b in range(0, 32, 16):
+            c2 = small[0, b : b + 16, :]
+            s2 = small[1, b : b + 16, :]
+            for v, value in ((0, c1 * c2 - s1 * s2), (1, s1 * c2 + c1 * s2)):
+                hi, lo = split(value)
+                rows = pl.ds(pl.multiple_of(v * half + a * 32 + b, 16), 16)
+                thi[rows, :] = hi
+                tlo[rows, :] = lo
+        return 0
+
+    lax.fori_loop(0, half // 32, build_square, 0)
+
+    width = half + LANE
+    wide_sub = lax.broadcasted_iota(jnp.int32, (SUB, width), 0)
+    wide_lane = lax.broadcasted_iota(jnp.int32, (SUB, width), 1)
+    lane = lax.broadcasted_iota(jnp.int32, (SUB, LANE), 1)
+    lane_sign = jnp.where(lane % 2 == 0, 1.0, -1.0).astype(f32)
+    edge = jnp.logical_or(wide_lane == 0, wide_lane == half)
+    scale = jnp.where(edge, -1.0, -2.0) * (1.0 / (n_y * n_y))
+    wide = (lax.broadcasted_iota(jnp.int32, (1, x_rows), 1) % 2).astype(f32) * -2.0 + 1.0
+    mid_copy.wait()
+
+    @pl.when(me == 0)
+    def _():
+        zero_copy.wait_send()
+
+    @pl.when(me == hdev)
+    def _():
+        zero_copy.wait_recv()
+
+    def all_of(buf, sem_s, sem_r):
+        return pltpu.make_async_remote_copy(
+            src_ref=buf, dst_ref=buf, send_sem=sem_s, recv_sem=sem_r,
+            device_id=at((me + 1) % devices), device_id_type=MESH,
+        )
+
+    def second(j, _):
+        top = jnp.logical_and(wide_sub == 0, j == 0)
+        use_mid = jnp.logical_and(top, me < hdev)
+        use_zero = jnp.logical_and(top, me == hdev)
+        wsc[...] = jnp.where(use_zero, scale, 2.0 * scale)
+        k_copy(j).wait()
+
+        def prep(i, _):
+            w = wsc[...]
+            value = jnp.where(use_mid, kmid[i], kre[i, :, 0:width])
+            other = jnp.where(use_zero, kzero[i], value)
+            for ref, k in ((kre, value * w), (kim, other * w)):
+                ref[i, :, 0:width] = k
+                ref[i, :, width : width + LANE] = jnp.where(lane == 0, k[:, half:width], k[:, 0:LANE])
+            return 0
+
+        lax.fori_loop(0, kre.shape[0], prep, 0)
+
+        for c in range(n_comp):
+            all_of(fs.at[j, c, pl.ds(0, devices - 1)], fsend.at[j, c], frecv.at[j, c]).wait_send()
+        for c in range(n_comp):
+            all_of(fr.at[j, c, pl.ds(0, devices - 1)], fsend.at[j, c], frecv.at[j, c]).wait_recv()
+
+        for h in range(2):
+            for s in range(n_layer):
+                for c in range(n_comp):
+                    row = h * m_rows + s * group + c * 2 * SUB
+                    for q in range(hrow):
+                        hi, lo = split(fr[j, c, s * n_row + h * hrow + q])
+                        ahi[row : row + 2 * SUB, q * x_rows : (q + 1) * x_rows] = hi
+                        alo[row : row + 2 * SUB, q * x_rows : (q + 1) * x_rows] = lo
+
+        lane2 = lax.broadcasted_iota(jnp.int32, (1, 256), 1)
+        sign2 = jnp.where(lane2 % 2 == 0, 1.0, -1.0).astype(f32)
+
+        def along(n, _):
+            cols = pl.ds(pl.multiple_of(n * 256, 256), 256)
+            for v in range(2):
+                rows = pl.ds(v * half, half)
+                p = dot(ahi[...], thi[rows, cols]) + dot(alo[...], thi[rows, cols]) + dot(ahi[...], tlo[rows, cols])
+                z[v, :, cols] = p[:m_rows] + sign2 * p[m_rows:]
+            return 0
+
+        lax.fori_loop(0, half // 256, along, 0)
+
+        def nyquist(i, _):
+            lo_rows = pl.ds(pl.multiple_of(i * 2 * SUB, 2 * SUB), 2 * SUB)
+            hi_rows = pl.ds(pl.multiple_of(m_rows + i * 2 * SUB, 2 * SUB), 2 * SUB)
+            a = ahi[lo_rows, :].astype(f32) + alo[lo_rows, :].astype(f32)
+            b = ahi[hi_rows, :].astype(f32) + alo[hi_rows, :].astype(f32)
+            both = a + b
+            signs = lax.broadcasted_iota(jnp.int32, both.shape, 1) % 2
+            total = jnp.sum(jnp.where(signs == 0, both, -both), axis=1, keepdims=True)
+            old = z[1, lo_rows, 0:LANE]
+            first_lane = lax.broadcasted_iota(jnp.int32, old.shape, 1) == 0
+            z[1, lo_rows, 0:LANE] = jnp.where(first_lane, total, old)
+            return 0
+
+        lax.fori_loop(0, m_rows // (2 * SUB), nyquist, 0)
+
+        def point(t, _):
+            cols = pl.ds(pl.multiple_of(t * LANE, LANE), LANE)
+            side = pl.ds(pl.multiple_of(jnp.where(t == 0, n_tile + 1, t) * LANE, LANE), LANE)
+            for target in range(n_layer):
+                total = None
+                for s in range(n_layer):
+                    o = (target - s + n_layer - 1) * 6
+
+                    def k(part, v, ri):
+                        return (kre, kim)[ri][o + part, :, (cols, side)[v]]
+
+                    def zz(v, c, ri):
+                        row = s * group + c * 2 * SUB + ri * SUB
+                        return z[v, row : row + SUB, cols]
+
+                    x = [[[zz(v, c, ri) for ri in range(2)] for c in range(3)] for v in range(2)]
+                    diag = [[[k(c, v, ri) for ri in range(2)] for v in range(2)] for c in range(3)]
+                    k3 = k(3, 0, 0)
+                    k4 = [k(4, 0, 0), k(4, 0, 1)]
+                    k5 = [k(5, 0, 0), k(5, 1, 0)]
+                    new = []
+                    for v in range(2):
+                        g = -1.0 if v else 1.0
+                        w = 1 - v
+                        own, opp = x[v], x[w]
+                        swap = ((1.0, 1), (-1.0, 0))
+                        for ri in range(2):
+                            sg, rj = swap[ri]
+                            b3 = (g * sg) * k3 if g * sg < 0 else k3
+                            b4 = -k4[ri] if v else k4[ri]
+                            b5 = -k5[v] if ri == 0 else k5[v]
+                            new.append(diag[0][v][ri] * own[0][ri] + b3 * opp[1][rj] + b4 * opp[2][ri])
+                            new.append(b3 * opp[0][rj] + diag[1][v][ri] * own[1][ri] + b5 * own[2][rj])
+                            new.append(b4 * opp[0][ri] + b5 * own[1][rj] + diag[2][v][ri] * own[2][ri])
+                    total = new if total is None else [a + b for a, b in zip(total, new)]
+                for v in range(2):
+                    out_cols = pl.ds(pl.multiple_of(v * half + t * LANE, LANE), LANE)
+                    for c in range(3):
+                        both = jnp.concatenate([total[v * 6 + c], total[v * 6 + 3 + c]], axis=0)
+                        hi, lo = split(both)
+                        sg = jnp.concatenate([lane_sign, lane_sign], axis=0)
+                        row = target * group + c * 2 * SUB
+                        for h in range(2):
+                            rows = pl.ds(h * m_rows + row, 2 * SUB)
+                            bhi[rows, out_cols] = hi if h == 0 else (hi.astype(f32) * sg).astype(bf16)
+                            blo[rows, out_cols] = lo if h == 0 else (lo.astype(f32) * sg).astype(bf16)
+            return 0
+
+        lax.fori_loop(0, n_tile, point, 0)
+
+        @pl.when(j < n_chunk - 1)
+        def _():
+            k_copy(j + 1).start()
+
+        def back(q, _):
+            cols = pl.ds(pl.multiple_of(q * x_rows, x_rows), x_rows)
+            p = dot(bhi[...], thi[:, cols]) + dot(blo[...], thi[:, cols]) + dot(bhi[...], tlo[:, cols])
+            edge_col = bhi[:, half : half + LANE].astype(f32) + blo[:, half : half + LANE].astype(f32)
+            p = p + edge_col[:, 0:1] * wide
+            for h in range(2):
+                for target in range(n_layer):
+                    for c in range(n_comp):
+                        row = h * m_rows + target * group + c * 2 * SUB
+                        fs[j, c, target * n_row + h * hrow + q] = p[row : row + 2 * SUB]
+
+            def send(k, _):
+                c = k // (2 * n_layer)
+                d = (k % n_layer) * n_row + (k // n_layer % 2) * hrow + q
+
+                @pl.when(d != me)
+                def _():
+                    pltpu.make_async_remote_copy(
+                        src_ref=fs.at[j, c, d], dst_ref=br.at[j, c, me], send_sem=bsend.at[j, c], recv_sem=brecv.at[j, c],
+                        device_id=at(d), device_id_type=MESH,
+                    ).start()
+
+                return 0
+
+            lax.fori_loop(0, n_comp * 2 * n_layer, send, 0)
+            return 0
+
+        lax.fori_loop(0, hrow, back, 0)
+        for c in range(n_comp):
+            br[j, c, me] = fs[j, c, me]
+        return 0
+
+    lax.fori_loop(0, n_chunk, second, 0)
+
+    def third(j, _):
+        build_rows(j)
+        for c in range(n_comp):
+            all_of(br.at[j, c, pl.ds(0, devices - 1)], bsend.at[j, c], brecv.at[j, c]).wait_recv()
+            turned = jnp.transpose(br[j, c].reshape(devices * 2 * SUB, x_rows))
+            hi, lo = split(turned)
+            mhi[c, :, 0 : devices * 2 * SUB] = hi
+            mlo[c, :, 0 : devices * 2 * SUB] = lo
+
+            def part(n, _):
+                cols = pl.ds(pl.multiple_of(n * 512, 512), 512)
+                hi = mhi[c, :, 0 : devices * 2 * SUB]
+                lo = mlo[c, :, 0 : devices * 2 * SUB]
+                value = dot(hi, lhi[:, cols]) + dot(lo, lhi[:, cols]) + dot(hi, llo[:, cols])
+
+                @pl.when(j == 0)
+                def _():
+                    acc[c, :, cols] = value
+
+                @pl.when(j > 0)
+                def _():
+                    acc[c, :, cols] = acc[c, :, cols] + value
+
+                return 0
+
+            lax.fori_loop(0, n_y // 512, part, 0)
+
+            @pl.when(j == n_chunk - 1)
+            def _():
+                pltpu.make_async_copy(acc.at[c], out_ref.at[c, 0], out_sem.at[c]).start()
+
+        return 0
+
+    lax.fori_loop(0, n_chunk, third, 0)
+    for j in range(n_chunk):
+        for c in range(n_comp):
+            all_of(fs.at[j, c, pl.ds(0, devices - 1)], bsend.at[j, c], brecv.at[j, c]).wait_send()
+    for c in range(n_comp):
+        pltpu.make_async_copy(acc.at[c], out_ref.at[c, 0], out_sem.at[c]).wait()
+
+
+def fused(magnet, kernel):
+    n_layer = lax.axis_size("layer")
+    n_row = lax.axis_size("row")
+    devices = n_row * n_layer
+    n_comp, _, x_rows, n_y = magnet.shape
+    n_off, n_part, block, n_x = kernel.shape
+    kept = block // 2
+    n_chunk = kept // SUB
+    half = n_y // 2
+    tables = base_tables(block, kept, devices, n_y)
+    group = 2 * SUB * n_comp
+    m_rows = n_layer * group
+    blocks = (n_chunk, n_comp, devices, 2 * SUB, x_rows)
+    vm, sem = pltpu.VMEM, pltpu.SemaphoreType.DMA
+    width = half + LANE
+    n_k = n_off * n_part
+    scratch = [
+        vm((n_comp, x_rows, n_y), f32),
+        vm((n_comp, x_rows, n_y), bf16), vm((n_comp, x_rows, n_y), bf16),
+        vm(blocks, f32), vm(blocks, f32), vm(blocks, f32),
+        vm((n_y, half), bf16), vm((n_y, half), bf16),
+        vm((devices * 2 * SUB, n_y), bf16), vm((devices * 2 * SUB, n_y), bf16),
+        vm((n_k, SUB, width + LANE), f32), vm((n_k, SUB, width + LANE), f32),
+        vm((n_k, SUB, width), f32), vm((n_k, SUB, width), f32),
+        vm((2 * m_rows, half), bf16), vm((2 * m_rows, half), bf16),
+        vm((2, m_rows, half), f32),
+        vm((2 * m_rows, n_y), bf16), vm((2 * m_rows, n_y), bf16),
+        vm((SUB, width), f32),
+        sem((n_comp,)), sem, sem, sem, sem,
+        *[sem((n_chunk, n_comp))] * 4, sem((n_comp,)),
+    ]
+    dims = (n_layer, n_row, n_comp, x_rows, n_y, kept, n_chunk)
+    anywhere = pl.BlockSpec(memory_space=pl.ANY)
+    return pl.pallas_call(
+        functools.partial(fused_kernel, dims),
+        out_shape=jax.ShapeDtypeStruct(magnet.shape, f32),
+        in_specs=[anywhere, anywhere] + [pl.BlockSpec(memory_space=pltpu.VMEM)] * 3,
+        out_specs=anywhere,
+        scratch_shapes=scratch,
+        compiler_params=pltpu.CompilerParams(
+            collective_id=0, has_side_effects=True, vmem_limit_bytes=67043328
+        ),
+    )(magnet, kernel.reshape(n_k, block, n_x), *[jnp.asarray(t) for t in tables])
+
+
+def fits(magnet, kernel):
+    n_layer = lax.axis_size("layer")
+    n_row = lax.axis_size("row")
+    x_rows, n_y = magnet.shape[2:]
+    block, n_x = kernel.shape[2:]
+    return (
+        n_x == n_y and n_x // 2 % 512 == 0 and x_rows % 256 == 0 and n_row % 2 == 0
+        and block % 32 == 0 and x_rows * n_row == n_x and kernel.shape[0] == 2 * n_layer - 1
+    )
+
+
+def local(magnet, kernel):
+    if fits(magnet, kernel):
+        return fused(magnet, kernel)
+    return general(magnet, kernel)
+
+
 def solution(mesh):
     in_specs = (P(None, "layer", "row", None), P(None, None, ("layer", "row"), None))
     out_specs = P(None, "layer", "row", None)

time: 527 us -> 292 us (0.55)
  Pallas kernels: 0 us -> 286 us
  matrix products: 209 us -> 0 us
  waiting for transfers between devices: 96.9 us -> 0 us
  local copies, waits for them, and re-layouts: 88.3 us -> 6.29 us
  other arithmetic: 81.6 us -> 0 us
  starting transfers between devices: 44.9 us -> 0 us
    pallas_call x0 -> x1, Pallas kernels: none -> 286 us  [fused(): pl.pallas_call(functools.partial(fused_kernel, dims), out_shape=jax.Shape...]
    dot_general x18 -> x0, matrix products: 209 us -> none  [dot(): return jnp.einsum(form, a, b, precision=high)]
    all_to_all x6 -> x0, waiting for transfers between devices: 96.9 us -> none  [the longest x3 71.4 us: local(): lax.all_to_all(rows.reshape(devices, 2 * kept, x_rows), axes, split_axis=...]
    all_to_all x6 -> x0, starting transfers between devices: 44.9 us -> none  [the longest x3 22.9 us: local(): lax.all_to_all(rows.reshape(devices, 2 * kept, x_rows), axes, split_axis=...]
    reshape x10 -> x0, local copies, waits for them, and re-layouts: 38.8 us -> none  [the longest x1 15.1 us: row_table(): return pair.reshape(devices * 2 * kept, length)]
    mul x27 -> x0, other arithmetic: 37.2 us -> none  [the longest x12 25 us: local(): real_rows.append(total_r * weight)]
    another operation x4 -> x0, local copies, waits for them, and re-layouts: 21.9 us -> none  [the longest x1 21 us: row_table(): pair = jnp.stack([c1 * c2 - s1 * s2, -(c1 * s2 + s1 * c2)], axis=1)]
    sub x7 -> x0, other arithmetic: 20.4 us -> none  [the longest x1 8.83 us: product_table(): cos = (c1 * c2 - s1 * s2).reshape(length, length)]
  transfers between devices with their start and end apart: 6 -> 0, of which waited for: 4 -> 0; matrix products, arithmetic and copies ran while one was open for 44% -> 0% of each run, Pallas kernels for 0% -> 0%
where the time goes in v1:
time: 292 us
  Pallas kernels  286 us (98%)
  local copies, waits for them, and re-layouts  6.29 us (2%)
    pallas_call x1, Pallas kernels, fused(): pl.pallas_call(functools.partial(fused_kernel, dims), out_shape=jax.Shape...  286 us
    unnamed x1, local copies, waits for them, and re-layouts  6.29 us

profile of v1, /device:TPU:13, one launch (start us, length us, event | category | flops | bytes accessed | tf_op | source)
XLA Modules:
  0.0 292.1 jit_solution(11558678801262039114)
XLA Ops:
  0.0 285.8 %shard_map.55 = f32[3,1,256,2048]{3,2,1,0:T(8,128)} custom-call(f32[3,1,256,2048]{3,2,1,0:T(8,128)} %mag_ref.1, f32[42,64,2048]{2,1,0:T(8,128)} %bitcast.1, f32[2,32,1024]{2,1,0:T(8,128)} %constant.6.clone.coarse, f32[2,32,1024]{2,1,0:T(8,128)} %constant.7.clone.small, f32[2,2,32,1024]{3,2,1,0:T(8,128)} %constant.8.clone.rowt), custom_call_target="tpu_custom_call" | custom-call | tf_op jit(solution)/shard_map/pallas_call | solution.py:524
  285.8 6.3 %copy.7 = f32[3,1,256,2048]{3,2,1,0:T(8,128)} copy(f32[3,1,256,2048]{3,2,1,0:T(8,128)} %shard_map.55) | data formatting | bytes 12582912

commit v2 on v1

--- a/solution.py
+++ b/solution.py
@@ -142,9 +142,9 @@
 
 
 def fused_kernel(
-    dims, mag_ref, ker_ref, coarse, small, rowt, out_ref,
-    acc, mhi, mlo, fs, fr, br, thi, tlo, lhi, llo, kre, kim, kmid, kzero, ahi, alo, z, bhi, blo, wsc,
-    mag_sem, k_sem, kmid_sem, zero_send, zero_recv, fsend, frecv, bsend, brecv, out_sem,
+    dims, mag_ref, ker_ref, coarse_ref, small_ref, rowt_ref, acc,
+    coarse, small, rowt, mhi, mlo, fs, fr, br, thi, tlo, lhi, llo, kre, kim, kmid, kzero, ahi, alo, z, bhi, blo, wsc,
+    mag_sem, tab_sem, k_sem, kmid_sem, zero_send, zero_recv, fsend, frecv, bsend, brecv,
 ):
     n_layer, n_row, n_comp, x_rows, n_y, kept, n_chunk = dims
     devices = n_layer * n_row
@@ -159,16 +159,17 @@
     r = lax.axis_index("row")
     me = l * n_row + r
 
+    side = r // hrow
+    inner = l * hrow + r % hrow
+    mine = side * hdev + inner
+
     def at(d):
         return (d // n_row, d % n_row)
 
+    def place(p):
+        return (p % hdev // hrow, p // hdev * hrow + p % hrow)
+
     barrier = pltpu.get_barrier_semaphore()
-
-    def greet(k, _):
-        pl.semaphore_signal(barrier, inc=1, device_id=at((me + k) % devices), device_id_type=MESH)
-        return 0
-
-    lax.fori_loop(1, devices, greet, 0)
 
     def mag_copy(c):
         return pltpu.make_async_copy(mag_ref.at[c, 0], acc.at[c], mag_sem.at[c])
@@ -177,8 +178,13 @@
         src = ker_ref.at[:, pl.ds(pl.multiple_of(j * SUB, SUB), SUB), pl.ds(0, half + LANE)]
         return pltpu.make_async_copy(src, kre.at[:, :, pl.ds(0, half + LANE)], k_sem)
 
+    tables = ((rowt_ref, rowt), (coarse_ref, coarse), (small_ref, small))
+    tab_copies = [pltpu.make_async_copy(src, dst, tab_sem.at[i]) for i, (src, dst) in enumerate(tables)]
+    tab_copies[0].start()
+    tab_copies[1].start()
     for c in range(n_comp):
         mag_copy(c).start()
+    tab_copies[2].start()
     k_copy(0).start()
     mid_copy = pltpu.make_async_copy(ker_ref.at[:, pl.ds(kept, SUB), pl.ds(0, half + LANE)], kmid, kmid_sem)
     mid_copy.start()
@@ -187,13 +193,22 @@
         send_sem=zero_send, recv_sem=zero_recv, device_id=at((me + hdev) % devices), device_id_type=MESH,
     )
 
+    def greet(k, _):
+        pl.semaphore_signal(barrier, inc=1, device_id=at((me + k) % devices), device_id_type=MESH)
+        return 0
+
+    lax.fori_loop(1, devices, greet, 0)
+    tab_copies[0].wait()
+    tab_copies[1].wait()
+
     sub = lax.broadcasted_iota(jnp.int32, (SUB, half), 0)
     odd_row = jnp.where(sub % 2 == 0, 1.0, -1.0).astype(f32)
 
-    def build_rows(j):
+    def build_rows(j, h):
         rows = pl.ds(pl.multiple_of(j * SUB, SUB), SUB)
 
-        def body(e, _):
+        def body(i, _):
+            e = i // hrow * n_row + h * hrow + i % hrow
             c1 = coarse[0, pl.ds(e * step, 1), :]
             s1 = coarse[1, pl.ds(e * step, 1), :]
             for v in range(2):
@@ -207,58 +222,77 @@
                 both = jnp.concatenate([top, low], axis=0)
                 sign = jnp.concatenate([odd_row, odd_row], axis=0)
                 hi, lo = split(both)
-                at_row = pl.ds(pl.multiple_of((v * hdev + e) * 2 * SUB, 2 * SUB), 2 * SUB)
+                p = h * hdev + v * (hdev // 2) + i
+                at_row = pl.ds(pl.multiple_of(p * 2 * SUB, 2 * SUB), 2 * SUB)
                 lhi[at_row, 0:half] = hi
                 llo[at_row, 0:half] = lo
                 lhi[at_row, half : 2 * half] = (hi.astype(f32) * sign).astype(bf16)
                 llo[at_row, half : 2 * half] = (lo.astype(f32) * sign).astype(bf16)
             return 0
 
-        lax.fori_loop(0, hdev, body, 0)
+        lax.fori_loop(0, hdev // 2, body, 0)
+
+    def half_rows(h):
+        return pl.ds(pl.multiple_of(h * hdev * 2 * SUB, hdev * 2 * SUB), hdev * 2 * SUB)
+
+    def push(src, dst, j, c, h, ssem, rsem):
+        def send(k, _):
+            p = h * hdev + (inner + k) % hdev
+
+            @pl.when(p != mine)
+            def _():
+                pltpu.make_async_remote_copy(
+                    src_ref=src.at[j, c, p], dst_ref=dst.at[j, c, mine],
+                    send_sem=ssem.at[j, c, h], recv_sem=rsem.at[j, c, side],
+                    device_id=place(p), device_id_type=MESH,
+                ).start()
+
+            return 0
+
+        lax.fori_loop(0, hdev, send, 0)
 
     def first(j, _):
-        build_rows(j)
+        for near in range(2):
+            h = (side + 1 + near) % 2
+            build_rows(j, h)
+            for c in range(n_comp):
+                if near == 0:
+
+                    @pl.when(j == 0)
+                    def _():
+                        mag_copy(c).wait()
+
+                        def body(i, _):
+                            rows = pl.ds(pl.multiple_of(i * 16, 16), 16)
+                            hi, lo = split(acc[c, rows, :])
+                            mhi[c, rows, :] = hi
+                            mlo[c, rows, :] = lo
+                            return 0
+
+                        lax.fori_loop(0, x_rows // 16, body, 0)
+
+                rows = half_rows(h)
+                value = dot_t(lhi[rows, :], mhi[c]) + dot_t(llo[rows, :], mhi[c]) + dot_t(lhi[rows, :], mlo[c])
+                fs[j, c, pl.ds(h * hdev, hdev)] = value.reshape(hdev, 2 * SUB, x_rows)
+
+                if c == 0 and near == 0:
+
+                    @pl.when(j == 0)
+                    def _():
+                        pl.semaphore_wait(barrier, devices - 1)
+
+                push(fs, fr, j, c, h, fsend, frecv)
         for c in range(n_comp):
-
-            @pl.when(j == 0)
-            def _():
-                mag_copy(c).wait()
-
-                def body(i, _):
-                    rows = pl.ds(pl.multiple_of(i * 16, 16), 16)
-                    hi, lo = split(acc[c, rows, :])
-                    mhi[c, rows, :] = hi
-                    mlo[c, rows, :] = lo
-                    return 0
-
-                lax.fori_loop(0, x_rows // 16, body, 0)
-
-            value = dot_t(lhi[...], mhi[c]) + dot_t(llo[...], mhi[c]) + dot_t(lhi[...], mlo[c])
-            fs[j, c] = value.reshape(devices, 2 * SUB, x_rows)
-
-            if c == 0:
-
-                @pl.when(j == 0)
-                def _():
-                    pl.semaphore_wait(barrier, devices - 1)
-
-                    @pl.when(me == 0)
-                    def _():
-                        zero_copy.start()
-
-            def send(k, _):
-                d = (me + k) % devices
-                pltpu.make_async_remote_copy(
-                    src_ref=fs.at[j, c, d], dst_ref=fr.at[j, c, me], send_sem=fsend.at[j, c], recv_sem=frecv.at[j, c],
-                    device_id=at(d), device_id_type=MESH,
-                ).start()
-                return 0
-
-            lax.fori_loop(1, devices, send, 0)
-            fr[j, c, me] = fs[j, c, me]
+            fr[j, c, mine] = fs[j, c, mine]
         return 0
 
     lax.fori_loop(0, n_chunk, first, 0)
+
+    @pl.when(me == 0)
+    def _():
+        zero_copy.start()
+
+    tab_copies[2].wait()
 
     def build_square(a, _):
         c1 = coarse[0, pl.ds(a, 1), :]
@@ -293,11 +327,16 @@
     def _():
         zero_copy.wait_recv()
 
-    def all_of(buf, sem_s, sem_r):
+    def blocks_of(buf, j, c, h, ssem, rsem):
+        count = hdev - 1 if isinstance(h, str) else hdev
+        k = side if isinstance(h, str) else h
+        part = buf.at[j, c, pl.ds(0, count)]
         return pltpu.make_async_remote_copy(
-            src_ref=buf, dst_ref=buf, send_sem=sem_s, recv_sem=sem_r,
-            device_id=at((me + 1) % devices), device_id_type=MESH,
+            src_ref=part, dst_ref=part, send_sem=ssem.at[j, c, k], recv_sem=rsem.at[j, c, k],
+            device_id=place((mine + 1) % devices), device_id_type=MESH,
         )
+
+    far = 1 - side
 
     def second(j, _):
         top = jnp.logical_and(wide_sub == 0, j == 0)
@@ -318,16 +357,15 @@
         lax.fori_loop(0, kre.shape[0], prep, 0)
 
         for c in range(n_comp):
-            all_of(fs.at[j, c, pl.ds(0, devices - 1)], fsend.at[j, c], frecv.at[j, c]).wait_send()
-        for c in range(n_comp):
-            all_of(fr.at[j, c, pl.ds(0, devices - 1)], fsend.at[j, c], frecv.at[j, c]).wait_recv()
+            for h in ("near", far):
+                blocks_of(fr, j, c, h, fsend, frecv).wait()
 
         for h in range(2):
             for s in range(n_layer):
                 for c in range(n_comp):
                     row = h * m_rows + s * group + c * 2 * SUB
                     for q in range(hrow):
-                        hi, lo = split(fr[j, c, s * n_row + h * hrow + q])
+                        hi, lo = split(fr[j, c, h * hdev + s * hrow + q])
                         ahi[row : row + 2 * SUB, q * x_rows : (q + 1) * x_rows] = hi
                         alo[row : row + 2 * SUB, q * x_rows : (q + 1) * x_rows] = lo
 
@@ -361,14 +399,14 @@
 
         def point(t, _):
             cols = pl.ds(pl.multiple_of(t * LANE, LANE), LANE)
-            side = pl.ds(pl.multiple_of(jnp.where(t == 0, n_tile + 1, t) * LANE, LANE), LANE)
+            corner = pl.ds(pl.multiple_of(jnp.where(t == 0, n_tile + 1, t) * LANE, LANE), LANE)
             for target in range(n_layer):
                 total = None
                 for s in range(n_layer):
                     o = (target - s + n_layer - 1) * 6
 
                     def k(part, v, ri):
-                        return (kre, kim)[ri][o + part, :, (cols, side)[v]]
+                        return (kre, kim)[ri][o + part, :, (cols, corner)[v]]
 
                     def zz(v, c, ri):
                         row = s * group + c * 2 * SUB + ri * SUB
@@ -422,70 +460,60 @@
                 for target in range(n_layer):
                     for c in range(n_comp):
                         row = h * m_rows + target * group + c * 2 * SUB
-                        fs[j, c, target * n_row + h * hrow + q] = p[row : row + 2 * SUB]
-
-            def send(k, _):
-                c = k // (2 * n_layer)
-                d = (k % n_layer) * n_row + (k // n_layer % 2) * hrow + q
-
-                @pl.when(d != me)
-                def _():
-                    pltpu.make_async_remote_copy(
-                        src_ref=fs.at[j, c, d], dst_ref=br.at[j, c, me], send_sem=bsend.at[j, c], recv_sem=brecv.at[j, c],
-                        device_id=at(d), device_id_type=MESH,
-                    ).start()
-
-                return 0
-
-            lax.fori_loop(0, n_comp * 2 * n_layer, send, 0)
+                        fs[j, c, h * hdev + target * hrow + q] = p[row : row + 2 * SUB]
+
             return 0
 
         lax.fori_loop(0, hrow, back, 0)
+        for h in (side, far):
+            for c in range(n_comp):
+                push(fs, br, j, c, h, bsend, brecv)
         for c in range(n_comp):
-            br[j, c, me] = fs[j, c, me]
+            br[j, c, mine] = fs[j, c, mine]
         return 0
 
     lax.fori_loop(0, n_chunk, second, 0)
 
     def third(j, _):
-        build_rows(j)
-        for c in range(n_comp):
-            all_of(br.at[j, c, pl.ds(0, devices - 1)], bsend.at[j, c], brecv.at[j, c]).wait_recv()
-            turned = jnp.transpose(br[j, c].reshape(devices * 2 * SUB, x_rows))
-            hi, lo = split(turned)
-            mhi[c, :, 0 : devices * 2 * SUB] = hi
-            mlo[c, :, 0 : devices * 2 * SUB] = lo
-
-            def part(n, _):
-                cols = pl.ds(pl.multiple_of(n * 512, 512), 512)
-                hi = mhi[c, :, 0 : devices * 2 * SUB]
-                lo = mlo[c, :, 0 : devices * 2 * SUB]
-                value = dot(hi, lhi[:, cols]) + dot(lo, lhi[:, cols]) + dot(hi, llo[:, cols])
-
-                @pl.when(j == 0)
-                def _():
-                    acc[c, :, cols] = value
-
-                @pl.when(j > 0)
-                def _():
-                    acc[c, :, cols] = acc[c, :, cols] + value
-
-                return 0
-
-            lax.fori_loop(0, n_y // 512, part, 0)
-
-            @pl.when(j == n_chunk - 1)
-            def _():
-                pltpu.make_async_copy(acc.at[c], out_ref.at[c, 0], out_sem.at[c]).start()
-
+        for h in range(2):
+            build_rows(j, h)
+        depth = hdev * 2 * SUB
+        for name, h in (("near", side), (far, far)):
+            rows = half_rows(h)
+            for c in range(n_comp):
+                blocks_of(br, j, c, name, bsend, brecv).wait_recv()
+                turned = jnp.transpose(br[j, c, pl.ds(h * hdev, hdev)].reshape(depth, x_rows))
+                hi, lo = split(turned)
+                mhi[c, :, 0:depth] = hi
+                mlo[c, :, 0:depth] = lo
+
+                def part(n, _):
+                    cols = pl.ds(pl.multiple_of(n * 512, 512), 512)
+                    hi = mhi[c, :, 0:depth]
+                    lo = mlo[c, :, 0:depth]
+                    value = dot(hi, lhi[rows, cols]) + dot(lo, lhi[rows, cols]) + dot(hi, llo[rows, cols])
+                    if name == "near":
+
+                        @pl.when(j == 0)
+                        def _():
+                            acc[c, :, cols] = value
+
+                        @pl.when(j > 0)
+                        def _():
+                            acc[c, :, cols] = acc[c, :, cols] + value
+
+                    else:
+                        acc[c, :, cols] = acc[c, :, cols] + value
+                    return 0
+
+                lax.fori_loop(0, n_y // 512, part, 0)
         return 0
 
     lax.fori_loop(0, n_chunk, third, 0)
     for j in range(n_chunk):
         for c in range(n_comp):
-            all_of(fs.at[j, c, pl.ds(0, devices - 1)], bsend.at[j, c], brecv.at[j, c]).wait_send()
-    for c in range(n_comp):
-        pltpu.make_async_copy(acc.at[c], out_ref.at[c, 0], out_sem.at[c]).wait()
+            for h in ("near", far):
+                blocks_of(fs, j, c, h, bsend, brecv).wait_send()
 
 
 def fused(magnet, kernel):
@@ -505,7 +533,7 @@
     width = half + LANE
     n_k = n_off * n_part
     scratch = [
-        vm((n_comp, x_rows, n_y), f32),
+        *[vm(t.shape, f32) for t in tables],
         vm((n_comp, x_rows, n_y), bf16), vm((n_comp, x_rows, n_y), bf16),
         vm(blocks, f32), vm(blocks, f32), vm(blocks, f32),
         vm((n_y, half), bf16), vm((n_y, half), bf16),
@@ -516,21 +544,21 @@
         vm((2, m_rows, half), f32),
         vm((2 * m_rows, n_y), bf16), vm((2 * m_rows, n_y), bf16),
         vm((SUB, width), f32),
-        sem((n_comp,)), sem, sem, sem, sem,
-        *[sem((n_chunk, n_comp))] * 4, sem((n_comp,)),
+        sem((n_comp,)), sem((3,)), sem, sem, sem, sem,
+        *[sem((n_chunk, n_comp, 2))] * 4,
     ]
     dims = (n_layer, n_row, n_comp, x_rows, n_y, kept, n_chunk)
     anywhere = pl.BlockSpec(memory_space=pl.ANY)
     return pl.pallas_call(
         functools.partial(fused_kernel, dims),
-        out_shape=jax.ShapeDtypeStruct(magnet.shape, f32),
-        in_specs=[anywhere, anywhere] + [pl.BlockSpec(memory_space=pltpu.VMEM)] * 3,
-        out_specs=anywhere,
+        out_shape=pltpu.VMEM((n_comp, x_rows, n_y), f32),
+        in_specs=[anywhere] * 5,
+        out_specs=pl.BlockSpec(memory_space=pltpu.VMEM),
         scratch_shapes=scratch,
         compiler_params=pltpu.CompilerParams(
-            collective_id=0, has_side_effects=True, vmem_limit_bytes=67043328
+            collective_id=0, has_side_effects=True, vmem_limit_bytes=54 * 2**20
         ),
-    )(magnet, kernel.reshape(n_k, block, n_x), *[jnp.asarray(t) for t in tables])
+    )(magnet, kernel.reshape(n_k, block, n_x), *[jnp.asarray(t) for t in tables]).reshape(magnet.shape)
 
 
 def fits(magnet, kernel):
@@ -540,7 +568,7 @@
     block, n_x = kernel.shape[2:]
     return (
         n_x == n_y and n_x // 2 % 512 == 0 and x_rows % 256 == 0 and n_row % 2 == 0
-        and block % 32 == 0 and x_rows * n_row == n_x and kernel.shape[0] == 2 * n_layer - 1
+        and n_layer % 2 == 0 and block % 32 == 0 and x_rows * n_row == n_x and kernel.shape[0] == 2 * n_layer - 1
     )
 
 

time: 292 us -> 285 us (0.976)
  Pallas kernels: 286 us -> 280 us
  local copies, waits for them, and re-layouts: 6.29 us -> 2.71 us
    pallas_call x1, Pallas kernels: 286 us -> 280 us  [fused(): pl.pallas_call(functools.partial(fused_kernel, dims), out_shape=pltpu.VME...]
    unnamed x1, local copies, waits for them, and re-layouts: 6.29 us -> 2.71 us
where the time goes in v2:
time: 285 us; the launch traced here: 283 us
  Pallas kernels  280 us (98%)
    pallas_call x1, Pallas kernels, fused(): pl.pallas_call(functools.partial(fused_kernel, dims), out_shape=pltpu.VME...  280 us

profile of v2, /device:TPU:13, one launch (start us, length us, event | category | flops | bytes accessed | tf_op | source)
XLA Modules:
  0.0 282.6 jit_solution(318370113522345868)
XLA Ops:
  0.0 279.9 %shard_map.55 = f32[3,256,2048]{2,1,0:T(8,128)S(1)} custom-call(f32[3,1,256,2048]{3,2,1,0:T(8,128)} %mag_ref.1, f32[42,64,2048]{2,1,0:T(8,128)} %bitcast.5, f32[2,32,1024]{2,1,0:T(8,128)} %constant.6.clone.coarse_ref, f32[2,32,1024]{2,1,0:T(8,128)} %constant.7.clone.small_ref, f32[2,2,32,1024]{3,2,1,0:T(8,128)} %constant.8.clone.rowt_ref), custom_call_target="tpu_custom_call" | custom-call | tf_op jit(solution)/shard_map/pallas_call | solution.py:552
  279.9 2.7 copy.8

commit v3 on v2

--- a/solution.py
+++ b/solution.py
@@ -120,12 +120,13 @@
     half = length // 2
     fine = 32
     coarse = wave(np.arange(half // fine) * fine, length, half)
+    steps = wave(np.arange(devices // 2) * block, length, half)
     small = wave(np.arange(fine), length, half)
     low = np.arange(kept)
     low[0] = kept
     flip = (-1.0) ** np.arange(half)
     rows = np.stack([wave(low, length, half), wave(np.arange(kept), length, half) * flip])
-    return coarse.astype(np.float32), small.astype(np.float32), rows.astype(np.float32)
+    return [t.astype(np.float32) for t in (coarse, small, steps, rows)]
 
 
 def split(x):
@@ -142,8 +143,8 @@
 
 
 def fused_kernel(
-    dims, mag_ref, ker_ref, coarse_ref, small_ref, rowt_ref, acc,
-    coarse, small, rowt, mhi, mlo, fs, fr, br, thi, tlo, lhi, llo, kre, kim, kmid, kzero, ahi, alo, z, bhi, blo, wsc,
+    dims, mag_ref, ker_ref, coarse_ref, small_ref, steps_ref, rowt_ref, acc,
+    coarse, small, steps, rowt, mhi, mlo, fs, fr, br, thi, tlo, rows_hl, turn_hl, kre, kim, kmid, kzero, ahi, alo, z, bhi, blo, wsc,
     mag_sem, tab_sem, k_sem, kmid_sem, zero_send, zero_recv, fsend, frecv, bsend, brecv,
 ):
     n_layer, n_row, n_comp, x_rows, n_y, kept, n_chunk = dims
@@ -151,7 +152,6 @@
     half = n_y // 2
     hrow = n_row // 2
     hdev = devices // 2
-    step = half // hdev // 32
     group = 2 * SUB * n_comp
     m_rows = n_layer * group
     n_tile = half // LANE
@@ -169,35 +169,39 @@
     def place(p):
         return (p % hdev // hrow, p // hdev * hrow + p % hrow)
 
-    barrier = pltpu.get_barrier_semaphore()
-
-    def mag_copy(c):
-        return pltpu.make_async_copy(mag_ref.at[c, 0], acc.at[c], mag_sem.at[c])
+    head, tail = pl.ds(0, SUB), pl.ds(SUB, kept - SUB)
+    tables = [
+        (steps_ref, steps), (rowt_ref.at[:, :, head], rowt.at[:, :, head]),
+        (coarse_ref, coarse), (small_ref, small),
+    ]
+    if n_chunk > 1:
+        tables.append((rowt_ref.at[:, :, tail], rowt.at[:, :, tail]))
+    tab_copies = [pltpu.make_async_copy(src, dst, tab_sem.at[i]) for i, (src, dst) in enumerate(tables)]
+
+    def mag_copy(c, i):
+        rows = pl.ds(i * (x_rows // 2), x_rows // 2)
+        return pltpu.make_async_copy(mag_ref.at[c, 0, rows], acc.at[c, rows], mag_sem.at[c, i])
 
     def k_copy(j):
         src = ker_ref.at[:, pl.ds(pl.multiple_of(j * SUB, SUB), SUB), pl.ds(0, half + LANE)]
         return pltpu.make_async_copy(src, kre.at[:, :, pl.ds(0, half + LANE)], k_sem)
 
-    tables = ((rowt_ref, rowt), (coarse_ref, coarse), (small_ref, small))
-    tab_copies = [pltpu.make_async_copy(src, dst, tab_sem.at[i]) for i, (src, dst) in enumerate(tables)]
-    tab_copies[0].start()
-    tab_copies[1].start()
-    for c in range(n_comp):
-        mag_copy(c).start()
-    tab_copies[2].start()
-    k_copy(0).start()
     mid_copy = pltpu.make_async_copy(ker_ref.at[:, pl.ds(kept, SUB), pl.ds(0, half + LANE)], kmid, kmid_sem)
-    mid_copy.start()
     zero_copy = pltpu.make_async_remote_copy(
         src_ref=ker_ref.at[:, pl.ds(0, SUB), pl.ds(0, half + LANE)], dst_ref=kzero,
         send_sem=zero_send, recv_sem=zero_recv, device_id=at((me + hdev) % devices), device_id_type=MESH,
     )
 
-    def greet(k, _):
-        pl.semaphore_signal(barrier, inc=1, device_id=at((me + k) % devices), device_id_type=MESH)
-        return 0
-
-    lax.fori_loop(1, devices, greet, 0)
+    tab_copies[0].start()
+    tab_copies[1].start()
+    barrier = pltpu.get_barrier_semaphore()
+    layers = [(l + i) % n_layer for i in range(n_layer)]
+    rows_of = [(r + i) % n_row for i in range(n_row)]
+    for i in range(1, devices):
+        target = (layers[i // n_row], rows_of[i % n_row])
+        pl.semaphore_signal(barrier, inc=1, device_id=target, device_id_type=MESH)
+    mag_copy(0, 0).start()
+    mag_copy(0, 1).start()
     tab_copies[0].wait()
     tab_copies[1].wait()
 
@@ -209,8 +213,8 @@
 
         def body(i, _):
             e = i // hrow * n_row + h * hrow + i % hrow
-            c1 = coarse[0, pl.ds(e * step, 1), :]
-            s1 = coarse[1, pl.ds(e * step, 1), :]
+            c1 = steps[0, pl.ds(e, 1), :]
+            s1 = steps[1, pl.ds(e, 1), :]
             for v in range(2):
                 c2 = rowt[v, 0, rows, :]
                 s2 = rowt[v, 1, rows, :]
@@ -222,28 +226,25 @@
                 both = jnp.concatenate([top, low], axis=0)
                 sign = jnp.concatenate([odd_row, odd_row], axis=0)
                 hi, lo = split(both)
-                p = h * hdev + v * (hdev // 2) + i
-                at_row = pl.ds(pl.multiple_of(p * 2 * SUB, 2 * SUB), 2 * SUB)
-                lhi[at_row, 0:half] = hi
-                llo[at_row, 0:half] = lo
-                lhi[at_row, half : 2 * half] = (hi.astype(f32) * sign).astype(bf16)
-                llo[at_row, half : 2 * half] = (lo.astype(f32) * sign).astype(bf16)
+                at_row = pl.ds(pl.multiple_of((v * (hdev // 2) + i) * 2 * SUB, 2 * SUB), 2 * SUB)
+                for k, value in enumerate((hi, lo)):
+                    rows_hl[h, k, at_row, 0:half] = value
+                    rows_hl[h, k, at_row, half : 2 * half] = (value.astype(f32) * sign).astype(bf16)
             return 0
 
         lax.fori_loop(0, hdev // 2, body, 0)
 
-    def half_rows(h):
-        return pl.ds(pl.multiple_of(h * hdev * 2 * SUB, hdev * 2 * SUB), hdev * 2 * SUB)
-
-    def push(src, dst, j, c, h, ssem, rsem):
+    depth = hdev * 2 * SUB
+
+    def push(src, dst, j, c, h, ssem, rsem, some=slice(0, x_rows)):
         def send(k, _):
             p = h * hdev + (inner + k) % hdev
 
             @pl.when(p != mine)
             def _():
                 pltpu.make_async_remote_copy(
-                    src_ref=src.at[j, c, p], dst_ref=dst.at[j, c, mine],
-                    send_sem=ssem.at[j, c, h], recv_sem=rsem.at[j, c, side],
+                    src_ref=src.at[j, c, p, :, some], dst_ref=dst.at[j, c, mine, :, some],
+                    send_sem=ssem, recv_sem=rsem,
                     device_id=place(p), device_id_type=MESH,
                 ).start()
 
@@ -252,47 +253,70 @@
         lax.fori_loop(0, hdev, send, 0)
 
     def first(j, _):
+        @pl.when(j == 1)
+        def _():
+            for copy in tab_copies[4:]:
+                copy.wait()
+
         for near in range(2):
             h = (side + 1 + near) % 2
             build_rows(j, h)
+            if near == 0:
+
+                @pl.when(j == 0)
+                def _():
+                    for c in range(1, n_comp):
+                        mag_copy(c, 0).start()
+                        mag_copy(c, 1).start()
+                    for copy in tab_copies[2:]:
+                        copy.start()
+
             for c in range(n_comp):
-                if near == 0:
-
-                    @pl.when(j == 0)
-                    def _():
-                        mag_copy(c).wait()
-
-                        def body(i, _):
-                            rows = pl.ds(pl.multiple_of(i * 16, 16), 16)
-                            hi, lo = split(acc[c, rows, :])
-                            mhi[c, rows, :] = hi
-                            mlo[c, rows, :] = lo
-                            return 0
-
-                        lax.fori_loop(0, x_rows // 16, body, 0)
-
-                rows = half_rows(h)
-                value = dot_t(lhi[rows, :], mhi[c]) + dot_t(llo[rows, :], mhi[c]) + dot_t(lhi[rows, :], mlo[c])
-                fs[j, c, pl.ds(h * hdev, hdev)] = value.reshape(hdev, 2 * SUB, x_rows)
-
-                if c == 0 and near == 0:
-
-                    @pl.when(j == 0)
-                    def _():
-                        pl.semaphore_wait(barrier, devices - 1)
-
-                push(fs, fr, j, c, h, fsend, frecv)
+                pieces = 2 if c == 0 and near == 0 else 1
+                size = x_rows // pieces
+                for i in range(pieces):
+                    some = slice(i * size, (i + 1) * size)
+                    if near == 0:
+
+                        @pl.when(j == 0)
+                        def _():
+                            for k in range(2 // pieces):
+                                mag_copy(c, i + k).wait()
+
+                            def body(k, _):
+                                rows = pl.ds(pl.multiple_of(i * size + k * 16, 16), 16)
+                                hi, lo = split(acc[c, rows, :])
+                                mhi[c, rows, :] = hi
+                                mlo[c, rows, :] = lo
+                                return 0
+
+                            lax.fori_loop(0, size // 16, body, 0)
+
+                    value = dot_t(rows_hl[h].reshape(2 * depth, n_y), mhi[c, some])
+                    value = value[:depth] + value[depth:] + dot_t(rows_hl[h, 0], mlo[c, some])
+                    fs[j, c, pl.ds(h * hdev, hdev), :, some] = value.reshape(hdev, 2 * SUB, size)
+
+                    if c == 0 and near == 0 and i == 0:
+
+                        @pl.when(j == 0)
+                        def _():
+                            pl.semaphore_wait(barrier, devices - 1)
+
+                    push(fs, fr, j, c, h, fsend.at[j, h], frecv.at[j, side], some)
         for c in range(n_comp):
             fr[j, c, mine] = fs[j, c, mine]
         return 0
 
     lax.fori_loop(0, n_chunk, first, 0)
+    k_copy(0).start()
+    mid_copy.start()
 
     @pl.when(me == 0)
     def _():
         zero_copy.start()
 
     tab_copies[2].wait()
+    tab_copies[3].wait()
 
     def build_square(a, _):
         c1 = coarse[0, pl.ds(a, 1), :]
@@ -327,12 +351,11 @@
     def _():
         zero_copy.wait_recv()
 
-    def blocks_of(buf, j, c, h, ssem, rsem):
-        count = hdev - 1 if isinstance(h, str) else hdev
-        k = side if isinstance(h, str) else h
-        part = buf.at[j, c, pl.ds(0, count)]
+    def blocks_of(buf, j, name, ssem, rsem, c=None):
+        blocks = pl.ds(0, hdev - 1 if name == "near" else hdev)
+        part = buf.at[j, :, blocks] if c is None else buf.at[j, c, blocks]
         return pltpu.make_async_remote_copy(
-            src_ref=part, dst_ref=part, send_sem=ssem.at[j, c, k], recv_sem=rsem.at[j, c, k],
+            src_ref=part, dst_ref=part, send_sem=ssem, recv_sem=rsem,
             device_id=place((mine + 1) % devices), device_id_type=MESH,
         )
 
@@ -356,9 +379,8 @@
 
         lax.fori_loop(0, kre.shape[0], prep, 0)
 
-        for c in range(n_comp):
-            for h in ("near", far):
-                blocks_of(fr, j, c, h, fsend, frecv).wait()
+        for name, h in (("near", side), ("far", far)):
+            blocks_of(fr, j, name, fsend.at[j, h], frecv.at[j, h]).wait()
 
         for h in range(2):
             for s in range(n_layer):
@@ -467,31 +489,35 @@
         lax.fori_loop(0, hrow, back, 0)
         for h in (side, far):
             for c in range(n_comp):
-                push(fs, br, j, c, h, bsend, brecv)
+                push(fs, br, j, c, h, bsend.at[j, h], brecv.at[j, c, side])
         for c in range(n_comp):
             br[j, c, mine] = fs[j, c, mine]
         return 0
 
     lax.fori_loop(0, n_chunk, second, 0)
 
+    wide_part = n_y // 2
+
     def third(j, _):
         for h in range(2):
             build_rows(j, h)
-        depth = hdev * 2 * SUB
-        for name, h in (("near", side), (far, far)):
-            rows = half_rows(h)
+
+        @pl.when(j > 0)
+        def _():
+            blocks_of(fs, j - 1, "far", bsend.at[j - 1, far], brecv.at[j - 1, 0, far]).wait_send()
+
+        for name, h in (("near", side), ("far", far)):
             for c in range(n_comp):
-                blocks_of(br, j, c, name, bsend, brecv).wait_recv()
+                blocks_of(br, j, name, bsend.at[j, h], brecv.at[j, c, h], c).wait_recv()
                 turned = jnp.transpose(br[j, c, pl.ds(h * hdev, hdev)].reshape(depth, x_rows))
                 hi, lo = split(turned)
-                mhi[c, :, 0:depth] = hi
-                mlo[c, :, 0:depth] = lo
+                turn_hl[0:x_rows, :] = hi
+                turn_hl[x_rows : 2 * x_rows, :] = lo
 
                 def part(n, _):
-                    cols = pl.ds(pl.multiple_of(n * 512, 512), 512)
-                    hi = mhi[c, :, 0:depth]
-                    lo = mlo[c, :, 0:depth]
-                    value = dot(hi, lhi[rows, cols]) + dot(lo, lhi[rows, cols]) + dot(hi, llo[rows, cols])
+                    cols = pl.ds(pl.multiple_of(n * wide_part, wide_part), wide_part)
+                    value = dot(turn_hl[...], rows_hl[h, 0, :, cols])
+                    value = value[:x_rows] + value[x_rows:] + dot(turn_hl[0:x_rows, :], rows_hl[h, 1, :, cols])
                     if name == "near":
 
                         @pl.when(j == 0)
@@ -506,14 +532,13 @@
                         acc[c, :, cols] = acc[c, :, cols] + value
                     return 0
 
-                lax.fori_loop(0, n_y // 512, part, 0)
+                lax.fori_loop(0, n_y // wide_part, part, 0)
+            if name == "near":
+                blocks_of(fs, j, name, bsend.at[j, h], brecv.at[j, 0, h]).wait_send()
         return 0
 
     lax.fori_loop(0, n_chunk, third, 0)
-    for j in range(n_chunk):
-        for c in range(n_comp):
-            for h in ("near", far):
-                blocks_of(fs, j, c, h, bsend, brecv).wait_send()
+    blocks_of(fs, n_chunk - 1, "far", bsend.at[n_chunk - 1, far], brecv.at[n_chunk - 1, 0, far]).wait_send()
 
 
 def fused(magnet, kernel):
@@ -537,22 +562,22 @@
         vm((n_comp, x_rows, n_y), bf16), vm((n_comp, x_rows, n_y), bf16),
         vm(blocks, f32), vm(blocks, f32), vm(blocks, f32),
         vm((n_y, half), bf16), vm((n_y, half), bf16),
-        vm((devices * 2 * SUB, n_y), bf16), vm((devices * 2 * SUB, n_y), bf16),
+        vm((2, 2, devices * SUB, n_y), bf16), vm((2 * x_rows, devices * SUB), bf16),
         vm((n_k, SUB, width + LANE), f32), vm((n_k, SUB, width + LANE), f32),
         vm((n_k, SUB, width), f32), vm((n_k, SUB, width), f32),
         vm((2 * m_rows, half), bf16), vm((2 * m_rows, half), bf16),
         vm((2, m_rows, half), f32),
         vm((2 * m_rows, n_y), bf16), vm((2 * m_rows, n_y), bf16),
         vm((SUB, width), f32),
-        sem((n_comp,)), sem((3,)), sem, sem, sem, sem,
-        *[sem((n_chunk, n_comp, 2))] * 4,
+        sem((n_comp, 2)), sem((5,)), sem, sem, sem, sem,
+        *[sem((n_chunk, 2))] * 3, sem((n_chunk, n_comp, 2)),
     ]
     dims = (n_layer, n_row, n_comp, x_rows, n_y, kept, n_chunk)
     anywhere = pl.BlockSpec(memory_space=pl.ANY)
     return pl.pallas_call(
         functools.partial(fused_kernel, dims),
         out_shape=pltpu.VMEM((n_comp, x_rows, n_y), f32),
-        in_specs=[anywhere] * 5,
+        in_specs=[anywhere] * 6,
         out_specs=pl.BlockSpec(memory_space=pltpu.VMEM),
         scratch_shapes=scratch,
         compiler_params=pltpu.CompilerParams(

time: 285 us -> 283 us (level)
  no operation moved by 1% of the time
where the time goes in v3:
time: 283 us; the launch traced here: 280 us
  Pallas kernels  278 us (98%)
    pallas_call x1, Pallas kernels, fused(): pl.pallas_call(functools.partial(fused_kernel, dims), out_shape=pltpu.VME...  278 us

profile of v3, /device:TPU:13, one launch (start us, length us, event | category | flops | bytes accessed | tf_op | source)
XLA Modules:
  0.0 280.3 jit_solution(16924482410753169401)
XLA Ops:
  0.0 277.6 %shard_map.64 = f32[3,256,2048]{2,1,0:T(8,128)S(1)} custom-call(f32[3,1,256,2048]{3,2,1,0:T(8,128)} %mag_ref.1, f32[42,64,2048]{2,1,0:T(8,128)} %bitcast.5, f32[2,32,1024]{2,1,0:T(8,128)} %constant.8.clone.coarse_ref, f32[2,32,1024]{2,1,0:T(8,128)} %constant.9.clone.small_ref, f32[2,16,1024]{2,1,0:T(8,128)} %constant.10.clone.steps_ref, ...), custom_call_target="tpu_custom_call" | custom-call | tf_op jit(solution)/shard_map/pallas_call | solution.py:577
  277.6 2.7 copy.9
